TPU v7x, 32 devices: a whole 2x2x4 slice. The times are simulated.
32 devices in a mesh: dp: 4 (over z), rows: 8 (over y, x, core).
Axes of the slice: x: 2, y: 2, z: 4, core: 2. Of those that a mesh axis runs over, the one named last changes fastest.
Arguments:
- owners: int32 [32768, 1], P(('dp', 'rows')), may hold values from 0 to 31; in each aligned block of 1024 rows (0 to 1023, 1024 to 2047, ...) at most 128 rows name the same one
- offsets: int32 [32768], P(('dp', 'rows')), may hold values from 0 to 8191
- gradients: bfloat16 [32768, 128], P(('dp', 'rows')), may hold values from -6 to 6
- embedding: float32 [262144, 128], P(('dp', 'rows')), may hold values from -6 to 6
- adagrad_state: float32 [262144], P(('dp', 'rows')), may hold values from 0.05 to 2
- next_owners: int32 [32768, 1], P(('dp', 'rows')), may hold values from 0 to 31; in each aligned block of 1024 rows (0 to 1023, 1024 to 2047, ...) at most 128 rows name the same one
- next_offsets: int32 [32768], P(('dp', 'rows')), may hold values from 0 to 8191
Outputs:
- new_embedding: float32 [262144, 128], P(('dp', 'rows'))
- new_state: float32 [262144], P(('dp', 'rows'))
- next_rows: bfloat16 [32768, 128], P(('dp', 'rows'))
Inputs may be any that keep to these rules, and one draw needn't show every extreme that they name: `owners`: within the 1024 rows of one device, at most 128 rows name the same block. `next_owners`: within the 1024 rows of one device, at most 128 rows name the same block.
All inputs are finite; a program needn't handle non-finite values.
Results may differ from a plain program's by a relative error of at most 0.0013.
Values may be sent and summed in bfloat16 or wider, within the bound.
A program may use at most 64 MiB of HBM per device.

v0:
```python
import jax
import jax.numpy as jnp
from jax import lax
from jax.sharding import PartitionSpec as P


def assign_slots(owner_ids, active, devices):
    lookups = owner_ids.shape[0]
    one_hot = (
        (owner_ids[:, None] == jnp.arange(devices, dtype=jnp.int32)[None, :]) & active[:, None]
    ).astype(jnp.bfloat16)
    positions = jnp.arange(lookups, dtype=jnp.int32)
    earlier = (positions[:, None] > positions[None, :]).astype(jnp.bfloat16)
    ahead_count = jnp.dot(earlier, one_hot, preferred_element_type=jnp.float32)
    return jnp.take_along_axis(ahead_count, owner_ids[:, None], axis=1)[:, 0].astype(jnp.int32)


def on_device(owners, offsets, gradients, embedding, adagrad_state, next_owners, next_offsets):
    devices = lax.axis_size(("dp", "rows"))
    lookups = gradients.shape[0]
    columns = gradients.shape[1]
    owned_rows = embedding.shape[0]
    capacity = max(2, 4 * lookups // devices)
    owner_ids = owners[:, 0]
    active = jnp.ones((lookups,), bool)
    slot_ids = assign_slots(owner_ids, active, devices)
    target = jnp.where(active, owner_ids, devices)
    outgoing = (
        jnp.zeros((devices, capacity, columns), gradients.dtype)
        .at[target, slot_ids]
        .set(gradients, mode="drop")
    )
    slot_rows = (
        jnp.zeros((devices, capacity), jnp.int32).at[target, slot_ids].set(offsets, mode="drop")
    )
    incoming, incoming_rows = (
        lax.all_to_all(outgoing, ("dp", "rows"), split_axis=0, concat_axis=0, tiled=True),
        lax.all_to_all(slot_rows, ("dp", "rows"), split_axis=0, concat_axis=0, tiled=True),
    )
    incoming = incoming.reshape(-1, columns).astype(jnp.float32)
    incoming_rows = incoming_rows.reshape(-1)
    grad_sum = jnp.zeros((owned_rows, columns), jnp.float32).at[incoming_rows].add(incoming)
    new_state = adagrad_state + jnp.mean(grad_sum * grad_sum, axis=1)
    new_embedding = embedding - 0.5 * grad_sum / jnp.sqrt(new_state)[:, None]
    table_half = new_embedding.astype(jnp.bfloat16)
    wanted = next_owners[:, 0]
    next_slots = assign_slots(wanted, jnp.ones((lookups,), bool), devices)
    requests = jnp.zeros((devices, capacity), jnp.int32).at[wanted, next_slots].set(next_offsets)
    fetched = table_half[
        lax.all_to_all(requests, ("dp", "rows"), split_axis=0, concat_axis=0, tiled=True)
    ]
    returned = lax.all_to_all(fetched, ("dp", "rows"), split_axis=0, concat_axis=0, tiled=True)
    next_rows = returned[wanted, next_slots]
    return (new_embedding, new_state, next_rows)


def solution(mesh):
    in_specs = (
        P(("dp", "rows"), None),
        P(("dp", "rows")),
        P(("dp", "rows"), None),
        P(("dp", "rows"), None),
        P(("dp", "rows")),
        P(("dp", "rows"), None),
        P(("dp", "rows")),
    )
    out_specs = (P(("dp", "rows"), None), P(("dp", "rows")), P(("dp", "rows"), None))
    return jax.shard_map(
        on_device, mesh=mesh, in_specs=in_specs, out_specs=out_specs, check_vma=False
    )
```

profile of v0, /device:TPU:0, one launch (start us, length us, event | category | flops | bytes accessed | tf_op | source)
XLA Modules:
  0.0 175.6 jit_solution(6237955416011522801)
XLA Ops:
  0.6 0.0 copy-start.1
  0.6 0.0 copy-start.2
  0.7 0.7 compare_select_fusion.5
  1.4 0.7 fusion.26
  2.1 0.7 compare_select_fusion.3
  2.8 0.7 fusion.25
  3.5 1.3 fusion
  4.9 8.6 %gather_fusion.3 = f32[1024]{0:T(1024)S(1)} fusion(f32[1024,32]{0,1:T(8,128)S(1)} %fusion, s32[1024]{0:T(1024)S(1)} %bitcast.34), kind=kCustom, calls=%fused_computation.1.clone | custom fusion | bytes 16384 | tf_op jit(solution)/shard_map/jit(take_along_axis)/gather | solution.py:15
  13.5 0.0 copy-start.4
  13.5 0.0 copy-start.5
  13.5 0.0 copy-done.2
  13.6 0.0 copy-done.1
  13.6 0.6 fusion.1
  14.2 8.6 %gather_fusion.2 = f32[1024]{0:T(1024)S(1)} fusion(f32[1024,32]{0,1:T(8,128)S(1)} %fusion.1, s32[1024]{0:T(1024)S(1)} %bitcast.33), kind=kCustom, calls=%fused_computation.clone | custom fusion | bytes 16384 | tf_op jit(solution)/shard_map/jit(take_along_axis)/gather | solution.py:15
  22.9 0.0 copy-done.4
  22.9 0.1 and_reduce_fusion
  23.0 0.0 copy-done.5
  23.0 0.1 multiply_reduce_fusion.1
  23.2 5.1 %scatter_custom_fusion.3 = s32[4096]{0:T(1024)} fusion(s32[1024]{0:T(1024)S(1)} %broadcast_select_fusion, s32[1024]{0:T(1024)} %param.15, s32[]{:T(128)} %constant.17.clone.1), kind=kCustom, calls=%fused_computation.41 | custom fusion | bytes 16896
  28.2 7.3 %all-to-all-start.2 = ((s32[32,1,128]{2,1,0:T(1,128)}), s32[32,1,128]{2,1,0:T(1,128)S(1)}, u32[]{:S(2)}, u32[]{:S(2)}) async-start(s32[32,1,128]{2,1,0:T(1,128)} %bitcast.15), calls=%async_computation.2 | async-start | bytes 32768 | tf_op jit(solution)/shard_map/all_to_all | solution.py:50
  35.5 5.1 %scatter_custom_fusion.1 = s32[4096]{0:T(1024)} fusion(s32[1024]{0:T(1024)S(1)} %broadcast_select_fusion.1, s32[1024]{0:T(1024)} %param.10, s32[]{:T(128)} %constant.17.clone.1), kind=kCustom, calls=%fused_computation.43 | custom fusion | bytes 16896
  40.6 2.0 %all-to-all-done.2 = s32[32,1,128]{2,1,0:T(1,128)S(1)} async-done(((s32[32,1,128]{2,1,0:T(1,128)}), s32[32,1,128]{2,1,0:T(1,128)S(1)}, u32[]{:S(2)}, u32[]{:S(2)}) %all-to-all-start.2) | async-done | bytes 16416 | tf_op jit(solution)/shard_map/all_to_all | solution.py:50
  42.6 3.8 %all-to-all-start = ((s32[32,1,128]{2,1,0:T(1,128)}), s32[32,1,128]{2,1,0:T(1,128)S(1)}, u32[]{:S(2)}, u32[]{:S(2)}) async-start(s32[32,1,128]{2,1,0:T(1,128)} %bitcast.5), calls=%async_computation | async-start | bytes 32768 | tf_op jit(solution)/shard_map/all_to_all | solution.py:38
  46.4 4.6 %scatter_custom_fusion.2 = bf16[4096,128]{1,0:T(8,128)(2,1)} fusion(s32[1024]{0:T(1024)S(1)} %broadcast_select_fusion.1, bf16[1024,128]{1,0:T(8,128)(2,1)} %param.11, bf16[]{:T(256)} %constant.2.clone.1), kind=kCustom, calls=%fused_computation.16 | custom fusion | bytes 1049088
  51.1 2.5 %all-to-all-done = s32[32,1,128]{2,1,0:T(1,128)S(1)} async-done(((s32[32,1,128]{2,1,0:T(1,128)}), s32[32,1,128]{2,1,0:T(1,128)S(1)}, u32[]{:S(2)}, u32[]{:S(2)}) %all-to-all-start) | async-done | bytes 16416 | tf_op jit(solution)/shard_map/all_to_all | solution.py:38
  53.5 3.4 %all-to-all-start.1 = ((bf16[32,128,128]{2,1,0:T(8,128)(2,1)}), bf16[32,128,128]{2,1,0:T(8,128)(2,1)S(1)}, u32[]{:S(2)}, u32[]{:S(2)}) async-start(bf16[32,128,128]{2,1,0:T(8,128)(2,1)} %bitcast.8), calls=%async_computation.1 | async-start | bytes 2097152 | tf_op jit(solution)/shard_map/all_to_all | solution.py:37
  57.0 26.2 %all-to-all-done.1 = bf16[32,128,128]{2,1,0:T(8,128)(2,1)S(1)} async-done(((bf16[32,128,128]{2,1,0:T(8,128)(2,1)}), bf16[32,128,128]{2,1,0:T(8,128)(2,1)S(1)}, u32[]{:S(2)}, u32[]{:S(2)}) %all-to-all-start.1) | async-done | bytes 1048608 | tf_op jit(solution)/shard_map/all_to_all | solution.py:37
  83.1 0.0 copy-start.3
  83.1 28.8 %scatter_custom_fusion = f32[8192,128]{1,0:T(8,128)} fusion(s32[4096]{0:T(1024)S(1)} %bitcast.40, bf16[4096,128]{1,0:T(8,128)(2,1)S(1)} %bitcast.36, f32[]{:T(128)} %constant.16.clone.1), kind=kCustom, calls=%fused_computation.13 | custom fusion | flops 1048576 | bytes 5242884 | tf_op jit(solution)/shard_map/scatter-add | solution.py:42
  112.0 0.0 copy-start
  112.0 3.5 %multiply_reduce_fusion = f32[8192]{0:T(1024)S(1)} fusion(f32[8192,128]{1,0:T(8,128)} %scatter_custom_fusion), kind=kLoop, calls=%fused_computation.9 | loop fusion | flops 2088960 | bytes 4227072 | tf_op jit(solution)/shard_map/reduce_sum | solution.py:43
  115.5 0.0 copy-done.3
  115.5 0.6 fusion.24
  116.1 0.0 copy-done
  116.1 6.6 %fusion.23 = (bf16[8192,128]{1,0:T(8,128)(2,1)S(1)}, f32[8192,128]{1,0:T(8,128)}) fusion(f32[8192,128]{1,0:T(8,128)} %param.12, f32[8192]{0:T(1024)S(1)} %get-tuple-element.12, f32[8192,128]{1,0:T(8,128)S(1)} %copy-done), kind=kLoop, calls=%fused_computation.60 | loop fusion | flops 4194304 | bytes 14712832 | tf_op jit(solution)/shard_map/convert_element_type | solution.py:45
  122.7 12.1 %gather_fusion = bf16[4096,128]{1,0:T(8,128)(2,1)S(1)} fusion(bf16[8192,128]{1,0:T(8,128)(2,1)S(1)} %get-tuple-element.10, s32[4096]{0:T(1024)S(1)} %fusion.10), kind=kCustom, calls=%fused_computation.2 | custom fusion | bytes 2113536 | tf_op jit(solution)/shard_map/gather | solution.py:49
  134.8 30.2 %all_to_all.31 = bf16[32,128,128]{2,1,0:T(8,128)(2,1)S(1)} all-to-all(bf16[32,128,128]{2,1,0:T(8,128)(2,1)S(1)} %bitcast.35), channel_id=1, replica_groups=mesh['dp'=4,'rows'=8] {'dp','rows'}, dimensions={0} | all-to-all | bytes 2097152 | tf_op jit(solution)/shard_map/all_to_all | solution.py:52
  165.0 10.5 %gather_fusion.1 = bf16[1024,128]{1,0:T(8,128)(2,1)} fusion(bf16[32,128,128]{2,1,0:T(8,128)(2,1)S(1)} %all_to_all.31, s32[1024]{0:T(1024)S(1)} %bitcast.32), kind=kCustom, calls=%fused_computation.3 | custom fusion | bytes 532480 | tf_op jit(solution)/shard_map/gather | solution.py:53
  (9 shorter events, 0.1 us)
Async XLA Ops:
  0.6 13.0 %copy-start.1 = (s32[1024,1]{0,1:T(1,128)S(1)}, s32[1024,1]{0,1:T(1,128)}, u32[]{:S(2)}) copy-start(s32[1024,1]{0,1:T(1,128)} %param.9) | copy-start | bytes 12292
  0.6 12.9 %copy-start.2 = (s32[1024,1]{0,1:T(1,128)S(1)}, s32[1024,1]{0,1:T(1,128)}, u32[]{:S(2)}) copy-start(s32[1024,1]{0,1:T(1,128)} %param.14) | copy-start | bytes 12292
  13.5 9.4 %copy-start.4 = (s32[2]{0:T(128)S(1)}, s32[2]{0:T(128)}, u32[]{:S(2)}) copy-start(s32[2]{0:T(128)} %constant.12) | copy-start | bytes 28
  13.5 9.5 %copy-start.5 = (s32[2]{0:T(128)S(1)}, s32[2]{0:T(128)}, u32[]{:S(2)}) copy-start(s32[2]{0:T(128)} %constant.5) | copy-start | bytes 28
  28.2 14.4 %all-to-all-start.2 = ((s32[32,1,128]{2,1,0:T(1,128)}), s32[32,1,128]{2,1,0:T(1,128)S(1)}, u32[]{:S(2)}, u32[]{:S(2)}) async-start(s32[32,1,128]{2,1,0:T(1,128)} %bitcast.15), calls=%async_computation.2 | async-start | bytes 32768 | tf_op jit(solution)/shard_map/all_to_all | solution.py:50
  42.6 10.9 %all-to-all-start = ((s32[32,1,128]{2,1,0:T(1,128)}), s32[32,1,128]{2,1,0:T(1,128)S(1)}, u32[]{:S(2)}, u32[]{:S(2)}) async-start(s32[32,1,128]{2,1,0:T(1,128)} %bitcast.5), calls=%async_computation | async-start | bytes 32768 | tf_op jit(solution)/shard_map/all_to_all | solution.py:38
  53.5 29.6 %all-to-all-start.1 = ((bf16[32,128,128]{2,1,0:T(8,128)(2,1)}), bf16[32,128,128]{2,1,0:T(8,128)(2,1)S(1)}, u32[]{:S(2)}, u32[]{:S(2)}) async-start(bf16[32,128,128]{2,1,0:T(8,128)(2,1)} %bitcast.8), calls=%async_computation.1 | async-start | bytes 2097152 | tf_op jit(solution)/shard_map/all_to_all | solution.py:37
  83.1 32.4 %copy-start.3 = (f32[8192]{0:T(1024)S(1)}, f32[8192]{0:T(1024)}, u32[]{:S(2)}) copy-start(f32[8192]{0:T(1024)} %param.13) | copy-start | bytes 98308
  112.0 4.1 %copy-start = (f32[8192,128]{1,0:T(8,128)S(1)}, f32[8192,128]{1,0:T(8,128)}, u32[]{:S(2)}) copy-start(f32[8192,128]{1,0:T(8,128)} %scatter_custom_fusion) | copy-start | bytes 12582916
where the time goes:
time: 176 us
  local copies, waits for them, and re-layouts  54.7 us (31%)
  other arithmetic  42.7 us (24%)
  waiting for transfers between devices  30.7 us (17%)
  blocking collectives  30.2 us (17%)
  starting transfers between devices  14.5 us (8%)
  matrix products  1.95 us (1%)
    all_to_all x1, blocking collectives, on_device(): lax.all_to_all(fetched, ('dp', 'rows'), split_axis=0, concat_axis=0, tile...  30.2 us
    scatter-add x1, other arithmetic, on_device(): jnp.zeros((owned_rows, columns), jnp.float32).at[incoming_rows]  28.8 us
    all_to_all x1, waiting for transfers between devices, on_device(): lax.all_to_all(outgoing, ('dp', 'rows'), split_axis=0, concat_axis=0, til...  26.2 us
    gather x2, local copies, waits for them, and re-layouts, assign_slots(): jnp.take_along_axis(ahead_count, owner_ids[:, None], axis=1)[:, 0]  17.3 us
    unnamed x15, local copies, waits for them, and re-layouts  14.8 us
    gather x1, local copies, waits for them, and re-layouts, on_device(): table_half[lax.all_to_all(requests, ('dp', 'rows'), split_axis=0, concat_...  12.1 us
    gather x1, local copies, waits for them, and re-layouts, on_device(): next_rows = returned[wanted, next_slots]  10.5 us
    all_to_all x1, starting transfers between devices, on_device(): lax.all_to_all(requests, ('dp', 'rows'), split_axis=0, concat_axis=0, til...  7.32 us
  transfers between devices with their start and end apart: 3, of which 3 were waited for; matrix products, arithmetic and copies ran while one was open for 6% of the time, Pallas kernels for 0%

commit v1 on v0

v1 whole, which is shorter than its diff:
```python
import jax
import jax.numpy as jnp
from jax import lax
from jax.experimental import pallas as pl
from jax.experimental.pallas import tpu as pltpu
from jax.sharding import PartitionSpec as P

BANKS = 4
LANES = 128
BASE = 256


def place(owner_ids, offsets, devices, capacity):
    lookups = owner_ids.shape[0]
    one_hot = (owner_ids[:, None] == jnp.arange(devices, dtype=jnp.int32)[None, :]).astype(
        jnp.bfloat16
    )
    positions = jnp.arange(lookups, dtype=jnp.int32)
    earlier = (positions[:, None] > positions[None, :]).astype(jnp.bfloat16)
    ahead = jnp.dot(earlier, one_hot, preferred_element_type=jnp.float32)
    slot_ids = jnp.sum(ahead * one_hot.astype(jnp.float32), axis=1).astype(jnp.int32)
    in_slot = slot_ids[:, None] == jnp.arange(capacity, dtype=jnp.int32)[None, :]
    high = (offsets // BASE).astype(jnp.float32)[:, None]
    low = (offsets % BASE).astype(jnp.float32)[:, None]
    columns = jnp.concatenate(
        [jnp.where(in_slot, high, 0.0), jnp.where(in_slot, low, 0.0), jnp.where(in_slot, 1.0, 0.0)],
        axis=1,
    ).astype(jnp.bfloat16)
    table = lax.dot_general(
        one_hot, columns, (((0,), (0,)), ((), ())), preferred_element_type=jnp.float32
    ).astype(jnp.int32)
    high, low, used = jnp.split(table, 3, axis=1)
    return owner_ids * capacity + slot_ids, high * BASE + low, used


def update_kernel(
    rows_ref, wanted_ref, incoming_ref, embedding_ref, state_ref,
    new_embedding_ref, new_state_ref, fetched_ref,
    *scratch,
):
    banks = scratch[:BANKS]
    table, picked, in_sem, out_sems = scratch[BANKS:]
    owned = table.shape[0]
    slots = incoming_ref.shape[0]
    chunks = out_sems.shape[0]
    chunk = owned // chunks

    load = pltpu.make_async_copy(embedding_ref, table, in_sem)
    load.start()

    zero_rows = 64

    @pl.loop(0, owned // zero_rows)
    def _(step):
        for bank in banks:
            bank[pl.ds(pl.multiple_of(step * zero_rows, zero_rows), zero_rows), :] = jnp.zeros(
                (zero_rows, LANES), jnp.float32
            )

    group = 32

    @pl.loop(0, slots // group)
    def _(step):
        start = pl.multiple_of(step * group, group)
        block = incoming_ref[pl.ds(start, group), :].astype(jnp.float32)
        for first in range(0, group, BANKS):
            where = [rows_ref[start + first + k] for k in range(BANKS)]
            sums = [
                banks[k][pl.ds(where[k], 1), :] + block[first + k : first + k + 1, :]
                for k in range(BANKS)
            ]
            for k in range(BANKS):
                banks[k][pl.ds(where[k], 1), :] = sums[k]

    load.wait()
    for piece in range(chunks):

        @pl.loop(0, chunk // LANES)
        def _(step):
            tile = piece * (chunk // LANES) + step
            span = pl.ds(pl.multiple_of(tile * LANES, LANES), LANES)
            grad_sum = banks[0][span, :]
            for bank in banks[1:]:
                grad_sum = grad_sum + bank[span, :]
            mean = jnp.sum(grad_sum * grad_sum, axis=1, keepdims=True) * (1.0 / LANES)
            old = jnp.broadcast_to(state_ref[pl.ds(tile, 1), :], (LANES, LANES)).T
            state = old + mean
            new_state_ref[pl.ds(tile, 1), :] = state.T[0:1, :]
            table[span, :] = table[span, :] - 0.5 * grad_sum / jnp.sqrt(state)

        span = pl.ds(piece * chunk, chunk)
        pltpu.make_async_copy(
            table.at[span, :], new_embedding_ref.at[span, :], out_sems.at[piece]
        ).start()

    @pl.loop(0, slots // group)
    def _(step):
        start = pl.multiple_of(step * group, group)
        for k in range(group):
            picked[pl.ds(start + k, 1), :] = table[pl.ds(wanted_ref[start + k], 1), :]

    @pl.loop(0, slots // LANES)
    def _(step):
        span = pl.ds(pl.multiple_of(step * LANES, LANES), LANES)
        fetched_ref[span, :] = picked[span, :].astype(jnp.bfloat16)

    for piece in range(chunks):
        span = pl.ds(piece * chunk, chunk)
        pltpu.make_async_copy(
            table.at[span, :], new_embedding_ref.at[span, :], out_sems.at[piece]
        ).wait()


def update(rows, wanted, incoming, embedding, state):
    owned, columns = embedding.shape
    slots = incoming.shape[0]
    chunks = 8
    smem = pl.BlockSpec(memory_space=pltpu.SMEM)
    vmem = pl.BlockSpec(memory_space=pltpu.VMEM)
    hbm = pl.BlockSpec(memory_space=pl.ANY)
    new_embedding, new_state, fetched = pl.pallas_call(
        update_kernel,
        name="update",
        out_shape=(
            jax.ShapeDtypeStruct((owned, columns), jnp.float32),
            jax.ShapeDtypeStruct((owned // LANES, LANES), jnp.float32),
            jax.ShapeDtypeStruct((slots, columns), jnp.bfloat16),
        ),
        in_specs=[smem, smem, vmem, hbm, vmem],
        out_specs=(hbm, vmem, vmem),
        scratch_shapes=[pltpu.VMEM((owned + 8, columns), jnp.float32)] * BANKS
        + [
            pltpu.VMEM((owned, columns), jnp.float32),
            pltpu.VMEM((slots, columns), jnp.float32),
            pltpu.SemaphoreType.DMA,
            pltpu.SemaphoreType.DMA((chunks,)),
        ],
        compiler_params=pltpu.CompilerParams(vmem_limit_bytes=40 * 1024 * 1024),
    )(rows, wanted, incoming, embedding, state.reshape(owned // LANES, LANES))
    return new_embedding, new_state.reshape(owned), fetched


def on_device(owners, offsets, gradients, embedding, adagrad_state, next_owners, next_offsets):
    axes = ("dp", "rows")
    devices = lax.axis_size(axes)
    lookups, columns = gradients.shape
    owned_rows = embedding.shape[0]
    capacity = max(2, 4 * lookups // devices)
    slots = devices * capacity
    places, slot_rows, used = place(owners[:, 0], offsets, devices, capacity)
    next_places, requests, _ = place(next_owners[:, 0], next_offsets, devices, capacity)
    slot_rows = jnp.where(used > 0, slot_rows, owned_rows)
    ids = jnp.stack([slot_rows, requests], axis=1)
    ids = lax.all_to_all(ids, axes, split_axis=0, concat_axis=0, tiled=True)
    slot_index = jnp.arange(slots, dtype=jnp.int32)
    outgoing = jnp.dot(
        (slot_index[:, None] == places[None, :]).astype(jnp.bfloat16),
        gradients,
        preferred_element_type=jnp.float32,
    ).astype(jnp.bfloat16)
    incoming = lax.all_to_all(
        outgoing.reshape(devices, capacity, columns), axes, split_axis=0, concat_axis=0, tiled=True
    )
    new_embedding, new_state, fetched = update(
        ids[:, 0].reshape(-1), ids[:, 1].reshape(-1),
        incoming.reshape(slots, columns), embedding, adagrad_state,
    )
    returned = lax.all_to_all(
        fetched.reshape(devices, capacity, columns), axes, split_axis=0, concat_axis=0, tiled=True
    )
    next_rows = jnp.dot(
        (next_places[:, None] == slot_index[None, :]).astype(jnp.bfloat16),
        returned.reshape(slots, columns),
        preferred_element_type=jnp.float32,
    ).astype(jnp.bfloat16)
    return (new_embedding, new_state, next_rows)


def solution(mesh):
    in_specs = (
        P(("dp", "rows"), None),
        P(("dp", "rows")),
        P(("dp", "rows"), None),
        P(("dp", "rows"), None),
        P(("dp", "rows")),
        P(("dp", "rows"), None),
        P(("dp", "rows")),
    )
    out_specs = (P(("dp", "rows"), None), P(("dp", "rows")), P(("dp", "rows"), None))
    return jax.shard_map(
        on_device, mesh=mesh, in_specs=in_specs, out_specs=out_specs, check_vma=False
    )
```

time: 176 us -> 114 us (0.65)
  local copies, waits for them, and re-layouts: 54.7 us -> 2.89 us
  other arithmetic: 42.7 us -> 2.78 us
  blocking collectives: 30.2 us -> 0 us
  Pallas kernels: 0 us -> 26.6 us
  waiting for transfers between devices: 30.7 us -> 55.6 us
  matrix products: 1.95 us -> 11.2 us
    gather x4 -> x0, local copies, waits for them, and re-layouts: 40 us -> none  [the longest x2 17.3 us: assign_slots(): jnp.take_along_axis(ahead_count, owner_ids[:, None], axis=1)[:, 0]]
    all_to_all x1 -> x0, blocking collectives: 30.2 us -> none  [on_device(): lax.all_to_all(fetched, ('dp', 'rows'), split_axis=0, concat_axis=0, tile...]
    scatter-add x1 -> x0, other arithmetic: 28.8 us -> none  [on_device(): jnp.zeros((owned_rows, columns), jnp.float32).at[incoming_rows]]
    pallas_call x0 -> x1, Pallas kernels: none -> 26.6 us  [update(): pl.pallas_call(update_kernel, name='update', out_shape=(jax.ShapeDtypeStr...]
    all_to_all x3, waiting for transfers between devices: 30.7 us -> 55.6 us  [the longest x1 26.2 us: on_device(): lax.all_to_all(fetched.reshape(devices, capacity, columns), axes, split_a...]
    unnamed x15 -> x10, local copies, waits for them, and re-layouts: 14.8 us -> 2.22 us
    dot_general x2 -> x6, matrix products: 1.95 us -> 11.2 us  [the longest x1 3.92 us: on_device(): jnp.dot((slot_index[:, None] == places[None, :]).astype(jnp.bfloat16), gr...]
    convert_element_type x1 -> x4, other arithmetic: 6.6 us -> 1.41 us  [the longest x2 1.4 us: place(): high = (offsets // BASE).astype(jnp.float32)[:, None]]
  transfers between devices with their start and end apart: 3 -> 3, of which waited for: 3 -> 3; matrix products, arithmetic and copies ran while one was open for 6% -> 3% of each run, Pallas kernels for 0% -> 0%
where the time goes in v1:
time: 114 us; the launch traced here: 113 us
  waiting for transfers between devices  55.6 us (49%)
  Pallas kernels  26.6 us (23%)
  starting transfers between devices  13.4 us (12%)
  matrix products  11.2 us (10%)
  local copies, waits for them, and re-layouts  2.89 us (3%)
  other arithmetic  2.78 us (2%)
    pallas_call x1, Pallas kernels, update(): pl.pallas_call(update_kernel, name='update', out_shape=(jax.ShapeDtypeStr...  26.6 us
    all_to_all x1, waiting for transfers between devices, on_device(): lax.all_to_all(fetched.reshape(devices, capacity, columns), axes, split_a...  26.2 us
    all_to_all x1, waiting for transfers between devices, on_device(): lax.all_to_all(outgoing.reshape(devices, capacity, columns), axes, split_...  26.2 us
    all_to_all x1, starting transfers between devices, on_device(): ids = lax.all_to_all(ids, axes, split_axis=0, concat_axis=0, tiled=True)  7.32 us
    dot_general x1, matrix products, on_device(): jnp.dot((slot_index[:, None] == places[None, :]).astype(jnp.bfloat16), gr...  3.92 us
    dot_general x1, matrix products, on_device(): jnp.dot((next_places[:, None] == slot_index[None, :]).astype(jnp.bfloat16...  3.51 us
    all_to_all x1, starting transfers between devices, on_device(): lax.all_to_all(fetched.reshape(devices, capacity, columns), axes, split_a...  3.48 us
    all_to_all x1, waiting for transfers between devices, on_device(): ids = lax.all_to_all(ids, axes, split_axis=0, concat_axis=0, tiled=True)  3.29 us
  transfers between devices with their start and end apart: 3, of which 3 were waited for; matrix products, arithmetic and copies ran while one was open for 3% of the time, Pallas kernels for 0%

profile of v1, /device:TPU:0, one launch (start us, length us, event | category | flops | bytes accessed | tf_op | source)
XLA Modules:
  0.0 113.4 jit_solution(10388938963331381420)
XLA Ops:
  0.6 0.0 copy-start
  0.6 0.0 copy-start.4
  0.7 0.0 copy-start.3
  0.7 1.3 %fusion.11 = f32[1024]{0:T(1024)S(1)} fusion(s32[1024]{0:T(1024)} %bitcast.24), kind=kOutput, calls=%fused_computation.14 | convolution fusion | flops 68353024 | bytes 8192 | tf_op jit(solution)/shard_map/dot_general | solution.py:20
  2.0 1.3 %fusion.10 = f32[1024]{0:T(1024)S(1)} fusion(s32[1024]{0:T(1024)} %bitcast.27), kind=kOutput, calls=%fused_computation.13 | convolution fusion | flops 68353024 | bytes 8192 | tf_op jit(solution)/shard_map/dot_general | solution.py:20
  3.3 0.7 fusion.31
  4.0 0.7 fusion.33
  4.7 0.2 select_convert_fusion
  4.9 0.2 select_convert_fusion.3
  5.1 0.5 select_convert_fusion.5
  5.6 0.9 convolution_convert_fusion.1
  6.6 0.5 select_convert_fusion.2
  7.0 0.0 copy-done.4
  7.0 0.2 convolution_convert_fusion
  7.3 0.6 copy.10
  7.9 7.3 %all-to-all-start = ((s32[32,2,128]{2,1,0:T(2,128)}), s32[32,2,128]{2,1,0:T(2,128)S(1)}, u32[]{:S(2)}, u32[]{:S(2)}) async-start(s32[32,2,128]{2,1,0:T(2,128)} %copy.10), calls=%async_computation | async-start | bytes 65536 | tf_op jit(solution)/shard_map/all_to_all | solution.py:154
  15.3 0.0 copy-done.3
  15.3 0.0 copy-done
  15.3 0.0 copy-start.2
  15.3 3.9 %fusion.4 = bf16[4096,128]{1,0:T(8,128)(2,1)} fusion(bf16[1024,128]{1,0:T(8,128)(2,1)S(1)} %copy-done, s32[1024]{0:T(1024)S(1)} %multiply_add_fusion.1), kind=kOutput, calls=%fused_computation.6 | convolution fusion | flops 1078460416 | bytes 1314816 | tf_op jit(solution)/shard_map/dot_general | solution.py:156
  19.2 3.3 %all-to-all-done = s32[32,2,128]{2,1,0:T(2,128)S(1)} async-done(((s32[32,2,128]{2,1,0:T(2,128)}), s32[32,2,128]{2,1,0:T(2,128)S(1)}, u32[]{:S(2)}, u32[]{:S(2)}) %all-to-all-start) | async-done | bytes 32800 | tf_op jit(solution)/shard_map/all_to_all | solution.py:154
  22.5 2.6 %all-to-all-start.1 = ((bf16[32,128,128]{2,1,0:T(8,128)(2,1)}), bf16[32,128,128]{2,1,0:T(8,128)(2,1)S(1)}, u32[]{:S(2)}, u32[]{:S(2)}) async-start(bf16[32,128,128]{2,1,0:T(8,128)(2,1)} %bitcast.6), calls=%async_computation.1 | async-start | bytes 2097152 | tf_op jit(solution)/shard_map/all_to_all | solution.py:161
  25.2 26.2 %all-to-all-done.1 = bf16[32,128,128]{2,1,0:T(8,128)(2,1)S(1)} async-done(((bf16[32,128,128]{2,1,0:T(8,128)(2,1)}), bf16[32,128,128]{2,1,0:T(8,128)(2,1)S(1)}, u32[]{:S(2)}, u32[]{:S(2)}) %all-to-all-start.1) | async-done | bytes 1048608 | tf_op jit(solution)/shard_map/all_to_all | solution.py:161
  51.4 0.0 copy-done.2
  51.4 0.0 copy-start.1
  51.4 2.2 %copy-done.1 = f32[8192,128]{1,0:T(8,128)S(1)} copy-done((f32[8192,128]{1,0:T(8,128)S(1)}, f32[8192,128]{1,0:T(8,128)}, u32[]{:S(2)}) %copy-start.1) | copy-done | bytes 4194328
  53.6 26.6 %update.1 = (f32[8192,128]{1,0:T(8,128)}, f32[64,128]{1,0:T(8,128)}, bf16[4096,128]{1,0:T(8,128)(2,1)}) custom-call(s32[4096]{0:T(1024)S(1)} %bitcast.20, s32[4096]{0:T(1024)S(1)} %bitcast.19, bf16[4096,128]{1,0:T(8,128)(2,1)S(1)} %bitcast.18, f32[8192,128]{1,0:T(8,128)S(1)} %copy-done.1, f32[64,128]{1,0:T(8,128)S(1)} %bitcast.21), custom_call_target="tpu_custom_call" | custom-call | tf_op jit(solution)/shard_map/update/pallas_call | solution.py:121
  80.2 3.5 %all-to-all-start.2 = ((bf16[32,128,128]{2,1,0:T(8,128)(2,1)}), bf16[32,128,128]{2,1,0:T(8,128)(2,1)S(1)}, u32[]{:S(2)}, u32[]{:S(2)}) async-start(bf16[32,128,128]{2,1,0:T(8,128)(2,1)} %bitcast.12), calls=%async_computation.2 | async-start | bytes 2097152 | tf_op jit(solution)/shard_map/all_to_all | solution.py:168
  83.7 26.2 %all-to-all-done.2 = bf16[32,128,128]{2,1,0:T(8,128)(2,1)S(1)} async-done(((bf16[32,128,128]{2,1,0:T(8,128)(2,1)}), bf16[32,128,128]{2,1,0:T(8,128)(2,1)S(1)}, u32[]{:S(2)}, u32[]{:S(2)}) %all-to-all-start.2) | async-done | bytes 1048608 | tf_op jit(solution)/shard_map/all_to_all | solution.py:168
  109.9 3.5 %fusion.7 = bf16[1024,128]{1,0:T(8,128)(2,1)} fusion(bf16[4096,128]{1,0:T(8,128)(2,1)S(1)} %bitcast.22, s32[1024]{0:T(1024)S(1)} %bitcast.29), kind=kOutput, calls=%fused_computation.10 | convolution fusion | flops 1078067200 | bytes 1314816 | tf_op jit(solution)/shard_map/dot_general | solution.py:171
  (8 shorter events, 0.1 us)
Async XLA Ops:
  0.6 14.7 %copy-start = (bf16[1024,128]{1,0:T(8,128)(2,1)S(1)}, bf16[1024,128]{1,0:T(8,128)(2,1)}, u32[]{:S(2)}) copy-start(bf16[1024,128]{1,0:T(8,128)(2,1)} %param.9) | copy-start | bytes 786436
  0.6 6.4 %copy-start.4 = (s32[1024,1]{0,1:T(1,128)S(1)}, s32[1024,1]{0,1:T(1,128)}, u32[]{:S(2)}) copy-start(s32[1024,1]{0,1:T(1,128)} %param.12) | copy-start | bytes 12292
  0.7 14.6 %copy-start.3 = (s32[1024,1]{0,1:T(1,128)S(1)}, s32[1024,1]{0,1:T(1,128)}, u32[]{:S(2)}) copy-start(s32[1024,1]{0,1:T(1,128)} %param.7) | copy-start | bytes 12292
  7.9 14.6 %all-to-all-start = ((s32[32,2,128]{2,1,0:T(2,128)}), s32[32,2,128]{2,1,0:T(2,128)S(1)}, u32[]{:S(2)}, u32[]{:S(2)}) async-start(s32[32,2,128]{2,1,0:T(2,128)} %copy.10), calls=%async_computation | async-start | bytes 65536 | tf_op jit(solution)/shard_map/all_to_all | solution.py:154
  15.3 36.1 %copy-start.2 = (f32[8192]{0:T(1024)S(1)}, f32[8192]{0:T(1024)}, u32[]{:S(2)}) copy-start(f32[8192]{0:T(1024)} %param.11) | copy-start | bytes 98308
  22.5 28.8 %all-to-all-start.1 = ((bf16[32,128,128]{2,1,0:T(8,128)(2,1)}), bf16[32,128,128]{2,1,0:T(8,128)(2,1)S(1)}, u32[]{:S(2)}, u32[]{:S(2)}) async-start(bf16[32,128,128]{2,1,0:T(8,128)(2,1)} %bitcast.6), calls=%async_computation.1 | async-start | bytes 2097152 | tf_op jit(solution)/shard_map/all_to_all | solution.py:161
  51.4 2.2 %copy-start.1 = (f32[8192,128]{1,0:T(8,128)S(1)}, f32[8192,128]{1,0:T(8,128)}, u32[]{:S(2)}) copy-start(f32[8192,128]{1,0:T(8,128)} %embedding_ref.1) | copy-start | bytes 12582916
  80.2 29.7 %all-to-all-start.2 = ((bf16[32,128,128]{2,1,0:T(8,128)(2,1)}), bf16[32,128,128]{2,1,0:T(8,128)(2,1)S(1)}, u32[]{:S(2)}, u32[]{:S(2)}) async-start(bf16[32,128,128]{2,1,0:T(8,128)(2,1)} %bitcast.12), calls=%async_computation.2 | async-start | bytes 2097152 | tf_op jit(solution)/shard_map/all_to_all | solution.py:168

commit v2 on v1

--- a/solution.py
+++ b/solution.py
@@ -10,15 +10,23 @@
 BASE = 256
 
 
-def place(owner_ids, offsets, devices, capacity):
+def positions_of(owner_ids, next_ids, devices):
     lookups = owner_ids.shape[0]
-    one_hot = (owner_ids[:, None] == jnp.arange(devices, dtype=jnp.int32)[None, :]).astype(
-        jnp.bfloat16
-    )
-    positions = jnp.arange(lookups, dtype=jnp.int32)
-    earlier = (positions[:, None] > positions[None, :]).astype(jnp.bfloat16)
+    names = jnp.arange(devices, dtype=jnp.int32)[None, :]
+    one_hot = jnp.concatenate(
+        [owner_ids[:, None] == names, next_ids[:, None] == names], axis=1
+    ).astype(jnp.bfloat16)
+    index = jnp.arange(lookups, dtype=jnp.int32)
+    earlier = (index[:, None] > index[None, :]).astype(jnp.bfloat16)
     ahead = jnp.dot(earlier, one_hot, preferred_element_type=jnp.float32)
-    slot_ids = jnp.sum(ahead * one_hot.astype(jnp.float32), axis=1).astype(jnp.int32)
+    hits = ahead * one_hot.astype(jnp.float32)
+    slots = jnp.sum(hits[:, :devices], axis=1), jnp.sum(hits[:, devices:], axis=1)
+    return tuple(part.astype(jnp.int32) for part in slots)
+
+
+def slot_table(owner_ids, slot_ids, offsets, devices, capacity):
+    names = jnp.arange(devices, dtype=jnp.int32)[None, :]
+    one_hot = (owner_ids[:, None] == names).astype(jnp.bfloat16)
     in_slot = slot_ids[:, None] == jnp.arange(capacity, dtype=jnp.int32)[None, :]
     high = (offsets // BASE).astype(jnp.float32)[:, None]
     low = (offsets % BASE).astype(jnp.float32)[:, None]
@@ -28,27 +36,32 @@
     ).astype(jnp.bfloat16)
     table = lax.dot_general(
         one_hot, columns, (((0,), (0,)), ((), ())), preferred_element_type=jnp.float32
-    ).astype(jnp.int32)
-    high, low, used = jnp.split(table, 3, axis=1)
-    return owner_ids * capacity + slot_ids, high * BASE + low, used
+    )
+    return jnp.split(table, 3, axis=1)
 
 
 def update_kernel(
-    rows_ref, wanted_ref, incoming_ref, embedding_ref, state_ref,
+    rows_hbm, wanted_hbm, incoming_ref, embedding_ref, state_ref,
     new_embedding_ref, new_state_ref, fetched_ref,
     *scratch,
 ):
     banks = scratch[:BANKS]
-    table, picked, in_sem, out_sems = scratch[BANKS:]
+    table, picked, rows_ref, wanted_ref, in_sem, rows_sem, wanted_sem, out_sems = scratch[BANKS:]
     owned = table.shape[0]
-    slots = incoming_ref.shape[0]
+    slots = picked.shape[0]
+    blocks = incoming_ref.shape[0]
+    capacity = slots // blocks
     chunks = out_sems.shape[0]
     chunk = owned // chunks
 
+    rows_load = pltpu.make_async_copy(rows_hbm, rows_ref, rows_sem)
+    rows_load.start()
+    wanted_load = pltpu.make_async_copy(wanted_hbm, wanted_ref, wanted_sem)
+    wanted_load.start()
     load = pltpu.make_async_copy(embedding_ref, table, in_sem)
     load.start()
 
-    zero_rows = 64
+    zero_rows = 128
 
     @pl.loop(0, owned // zero_rows)
     def _(step):
@@ -57,12 +70,15 @@
                 (zero_rows, LANES), jnp.float32
             )
 
-    group = 32
-
-    @pl.loop(0, slots // group)
+    group = 32 if capacity % 32 == 0 else 8
+    per_block = capacity // group
+    rows_load.wait()
+
+    @pl.loop(0, blocks * per_block)
     def _(step):
         start = pl.multiple_of(step * group, group)
-        block = incoming_ref[pl.ds(start, group), :].astype(jnp.float32)
+        within = pl.multiple_of(lax.rem(step, per_block) * group, group)
+        block = incoming_ref[lax.div(step, per_block), pl.ds(within, group), :].astype(jnp.float32)
         for first in range(0, group, BANKS):
             where = [rows_ref[start + first + k] for k in range(BANKS)]
             sums = [
@@ -75,7 +91,7 @@
     load.wait()
     for piece in range(chunks):
 
-        @pl.loop(0, chunk // LANES)
+        @pl.loop(0, chunk // LANES, unroll=2)
         def _(step):
             tile = piece * (chunk // LANES) + step
             span = pl.ds(pl.multiple_of(tile * LANES, LANES), LANES)
@@ -86,12 +102,14 @@
             old = jnp.broadcast_to(state_ref[pl.ds(tile, 1), :], (LANES, LANES)).T
             state = old + mean
             new_state_ref[pl.ds(tile, 1), :] = state.T[0:1, :]
-            table[span, :] = table[span, :] - 0.5 * grad_sum / jnp.sqrt(state)
+            table[span, :] = table[span, :] - 0.5 * grad_sum * lax.rsqrt(state)
 
         span = pl.ds(piece * chunk, chunk)
         pltpu.make_async_copy(
             table.at[span, :], new_embedding_ref.at[span, :], out_sems.at[piece]
         ).start()
+
+    wanted_load.wait()
 
     @pl.loop(0, slots // group)
     def _(step):
@@ -113,11 +131,10 @@
 
 def update(rows, wanted, incoming, embedding, state):
     owned, columns = embedding.shape
-    slots = incoming.shape[0]
+    slots = rows.shape[0]
     chunks = 8
-    smem = pl.BlockSpec(memory_space=pltpu.SMEM)
     vmem = pl.BlockSpec(memory_space=pltpu.VMEM)
-    hbm = pl.BlockSpec(memory_space=pl.ANY)
+    hbm = pl.BlockSpec(memory_space=pltpu.HBM)
     new_embedding, new_state, fetched = pl.pallas_call(
         update_kernel,
         name="update",
@@ -126,16 +143,20 @@
             jax.ShapeDtypeStruct((owned // LANES, LANES), jnp.float32),
             jax.ShapeDtypeStruct((slots, columns), jnp.bfloat16),
         ),
-        in_specs=[smem, smem, vmem, hbm, vmem],
+        in_specs=[hbm, hbm, vmem, hbm, vmem],
         out_specs=(hbm, vmem, vmem),
         scratch_shapes=[pltpu.VMEM((owned + 8, columns), jnp.float32)] * BANKS
         + [
             pltpu.VMEM((owned, columns), jnp.float32),
             pltpu.VMEM((slots, columns), jnp.float32),
+            pltpu.SMEM((slots,), jnp.int32),
+            pltpu.SMEM((slots,), jnp.int32),
+            pltpu.SemaphoreType.DMA,
+            pltpu.SemaphoreType.DMA,
             pltpu.SemaphoreType.DMA,
             pltpu.SemaphoreType.DMA((chunks,)),
         ],
-        compiler_params=pltpu.CompilerParams(vmem_limit_bytes=40 * 1024 * 1024),
+        compiler_params=pltpu.CompilerParams(vmem_limit_bytes=50 * 1024 * 1024),
     )(rows, wanted, incoming, embedding, state.reshape(owned // LANES, LANES))
     return new_embedding, new_state.reshape(owned), fetched
 
@@ -147,24 +168,31 @@
     owned_rows = embedding.shape[0]
     capacity = max(2, 4 * lookups // devices)
     slots = devices * capacity
-    places, slot_rows, used = place(owners[:, 0], offsets, devices, capacity)
-    next_places, requests, _ = place(next_owners[:, 0], next_offsets, devices, capacity)
-    slot_rows = jnp.where(used > 0, slot_rows, owned_rows)
-    ids = jnp.stack([slot_rows, requests], axis=1)
-    ids = lax.all_to_all(ids, axes, split_axis=0, concat_axis=0, tiled=True)
+    owner_ids, next_ids = owners[:, 0], next_owners[:, 0]
+    slot_ids, next_slots = positions_of(owner_ids, next_ids, devices)
+    places = owner_ids * capacity + slot_ids
+    next_places = next_ids * capacity + next_slots
+    high, low, used = slot_table(owner_ids, slot_ids, offsets, devices, capacity)
+    next_high, next_low, _ = slot_table(next_ids, next_slots, next_offsets, devices, capacity)
+    high = jnp.where(used > 0, high, owned_rows // BASE)
+    ids = jnp.concatenate([high, low, next_high, next_low], axis=1).astype(jnp.bfloat16)
+    id_rows = 8 * -(-4 * capacity // (8 * columns))
+    ids = jnp.pad(ids, ((0, 0), (0, id_rows * columns - 4 * capacity)))
     slot_index = jnp.arange(slots, dtype=jnp.int32)
     outgoing = jnp.dot(
         (slot_index[:, None] == places[None, :]).astype(jnp.bfloat16),
         gradients,
         preferred_element_type=jnp.float32,
     ).astype(jnp.bfloat16)
-    incoming = lax.all_to_all(
-        outgoing.reshape(devices, capacity, columns), axes, split_axis=0, concat_axis=0, tiled=True
-    )
-    new_embedding, new_state, fetched = update(
-        ids[:, 0].reshape(-1), ids[:, 1].reshape(-1),
-        incoming.reshape(slots, columns), embedding, adagrad_state,
-    )
+    outgoing = jnp.concatenate(
+        [outgoing.reshape(devices, capacity, columns), ids.reshape(devices, id_rows, columns)], axis=1
+    )
+    incoming = lax.all_to_all(outgoing, axes, split_axis=0, concat_axis=0, tiled=True)
+    ids = incoming[:, capacity:].reshape(devices, id_rows * columns)[:, : 4 * capacity]
+    ids = ids.astype(jnp.int32).reshape(devices, 4, capacity)
+    rows = (ids[:, 0] * BASE + ids[:, 1]).reshape(-1)
+    wanted = (ids[:, 2] * BASE + ids[:, 3]).reshape(-1)
+    new_embedding, new_state, fetched = update(rows, wanted, incoming, embedding, adagrad_state)
     returned = lax.all_to_all(
         fetched.reshape(devices, capacity, columns), axes, split_axis=0, concat_axis=0, tiled=True
     )

time: 114 us -> 97.2 us (0.85)
  blocking collectives: 0 us -> 36.5 us
  waiting for transfers between devices: 55.6 us -> 26.2 us
  starting transfers between devices: 13.4 us -> 2.66 us
  Pallas kernels: 26.6 us -> 20.7 us
  matrix products: 11.2 us -> 7.5 us
  local copies, waits for them, and re-layouts: 2.89 us -> 0.1 us
    all_to_all x0 -> x1, blocking collectives: none -> 36.5 us  [on_device(): lax.all_to_all(outgoing, axes, split_axis=0, concat_axis=0, tiled=True)]
    all_to_all x2 -> x0, waiting for transfers between devices: 29.4 us -> none  [the longest x1 26.2 us: on_device(): lax.all_to_all(outgoing.reshape(devices, capacity, columns), axes, split_...]
    all_to_all x2 -> x0, starting transfers between devices: 9.97 us -> none  [the longest x1 7.32 us: on_device(): ids = lax.all_to_all(ids, axes, split_axis=0, concat_axis=0, tiled=True)]
    pallas_call x1, Pallas kernels: 26.6 us -> 20.7 us  [update(): pl.pallas_call(update_kernel, name='update', out_shape=(jax.ShapeDtypeStr...]
    dot_general x4 -> x3, matrix products: 3.76 us -> 1.04 us  [the longest x1 0.58 us: positions_of(): ahead = jnp.dot(earlier, one_hot, preferred_element_type=jnp.float32)]
    unnamed x10 -> x14, local copies, waits for them, and re-layouts: 2.22 us -> 0.06 us
    convert_element_type x4, other arithmetic: 1.41 us -> 0.04 us  [the longest x2 0.03 us: slot_table(): high = (offsets // BASE).astype(jnp.float32)[:, None]]
  transfers between devices with their start and end apart: 3 -> 1, of which waited for: 3 -> 1; matrix products, arithmetic and copies ran while one was open for 3% -> 0% of each run, Pallas kernels for 0% -> 0%
where the time goes in v2:
time: 97.2 us; the launch traced here: 96.9 us
  blocking collectives  36.5 us (38%)
  waiting for transfers between devices  26.2 us (27%)
  Pallas kernels  20.7 us (21%)
  matrix products  7.5 us (8%)
  starting transfers between devices  2.66 us (3%)
  other arithmetic  2.37 us (2%)
    all_to_all x1, blocking collectives, on_device(): lax.all_to_all(outgoing, axes, split_axis=0, concat_axis=0, tiled=True)  36.5 us
    all_to_all x1, waiting for transfers between devices, on_device(): lax.all_to_all(fetched.reshape(devices, capacity, columns), axes, split_a...  26.2 us
    pallas_call x1, Pallas kernels, update(): pl.pallas_call(update_kernel, name='update', out_shape=(jax.ShapeDtypeStr...  20.7 us
    dot_general x1, matrix products, on_device(): jnp.dot((next_places[:, None] == slot_index[None, :]).astype(jnp.bfloat16...  3.51 us
    dot_general x1, matrix products, on_device(): jnp.dot((slot_index[:, None] == places[None, :]).astype(jnp.bfloat16), gr...  2.95 us
    all_to_all x1, starting transfers between devices, on_device(): lax.all_to_all(fetched.reshape(devices, capacity, columns), axes, split_a...  2.66 us
  transfers between devices with their start and end apart: 1, of which 1 were waited for; matrix products, arithmetic and copies ran while one was open for 0% of the time, Pallas kernels for 0%

profile of v2, /device:TPU:0, one launch (start us, length us, event | category | flops | bytes accessed | tf_op | source)
XLA Modules:
  0.0 96.9 jit_solution(8030807254392708914)
XLA Ops:
  0.6 0.0 copy-start
  0.6 0.0 copy-start.2
  0.7 0.0 copy-start.4
  0.7 0.8 iota_compare_fusion.15
  1.5 0.0 copy-start.5
  1.5 0.6 fusion.7
  2.1 0.0 copy-start.3
  2.1 0.0 copy-done.2
  2.1 0.0 copy-done.4
  2.2 0.2 select_convert_fusion.3
  2.4 0.5 select_convert_fusion.5
  2.9 0.2 fusion.8
  3.1 0.0 copy-done.5
  3.2 0.2 select_convert_fusion
  3.4 0.5 select_convert_fusion.2
  3.8 0.0 copy-done.3
  3.8 0.2 fusion.14
  4.1 0.0 copy-done
  4.1 2.9 %fusion.4 = bf16[4096,128]{1,0:T(8,128)(2,1)S(1)} fusion(bf16[1024,128]{1,0:T(8,128)(2,1)S(1)} %copy-done, s32[1024]{0:T(1024)S(1)} %multiply_add_fusion.1), kind=kOutput, calls=%fused_computation.6 | convolution fusion | flops 1078460416 | bytes 1314816 | tf_op jit(solution)/shard_map/dot_general | solution.py:182
  7.1 0.0 copy-start.1
  7.1 0.1 pad_maximum_fusion
  7.2 36.5 %all_to_all.10.incoming_ref = bf16[32,136,128]{2,1,0:T(8,128)(2,1)S(1)} all-to-all(bf16[32,136,128]{2,1,0:T(8,128)(2,1)S(1)} %pad_maximum_fusion), channel_id=1, replica_groups=mesh['dp'=4,'rows'=8] {'dp','rows'}, dimensions={0} | all-to-all | bytes 2228224 | tf_op jit(solution)/shard_map/all_to_all | solution.py:190
  43.8 0.0 copy-done.1
  43.8 20.7 %update.1 = (f32[8192,128]{1,0:T(8,128)}, f32[64,128]{1,0:T(8,128)}, bf16[4096,128]{1,0:T(8,128)(2,1)}) custom-call(s32[4096]{0:T(1024)S(1)} %bitcast.21, s32[4096]{0:T(1024)S(1)} %bitcast.20, bf16[32,136,128]{2,1,0:T(8,128)(2,1)S(1)} %all_to_all.10.incoming_ref, f32[8192,128]{1,0:T(8,128)} %embedding_ref.1, f32[64,128]{1,0:T(8,128)S(1)} %bitcast.22), custom_call_target="tpu_custom_call" | custom-call | tf_op jit(solution)/shard_map/update/pallas_call | solution.py:138
  64.5 2.7 %all-to-all-start.1 = ((bf16[32,128,128]{2,1,0:T(8,128)(2,1)}), bf16[32,128,128]{2,1,0:T(8,128)(2,1)S(1)}, u32[]{:S(2)}, u32[]{:S(2)}) async-start(bf16[32,128,128]{2,1,0:T(8,128)(2,1)} %bitcast.9), calls=%async_computation.1 | async-start | bytes 2097152 | tf_op jit(solution)/shard_map/all_to_all | solution.py:196
  67.2 26.2 %all-to-all-done.1 = bf16[32,128,128]{2,1,0:T(8,128)(2,1)S(1)} async-done(((bf16[32,128,128]{2,1,0:T(8,128)(2,1)}), bf16[32,128,128]{2,1,0:T(8,128)(2,1)S(1)}, u32[]{:S(2)}, u32[]{:S(2)}) %all-to-all-start.1) | async-done | bytes 1048608 | tf_op jit(solution)/shard_map/all_to_all | solution.py:196
  93.4 3.5 %fusion.6 = bf16[1024,128]{1,0:T(8,128)(2,1)} fusion(bf16[4096,128]{1,0:T(8,128)(2,1)S(1)} %bitcast.23, s32[1024]{0:T(1024)S(1)} %bitcast.34), kind=kOutput, calls=%fused_computation.9 | convolution fusion | flops 1078067200 | bytes 1314816 | tf_op jit(solution)/shard_map/dot_general | solution.py:199
  (17 shorter events, 0.2 us)
Async XLA Ops:
  0.6 3.5 %copy-start = (bf16[1024,128]{1,0:T(8,128)(2,1)S(1)}, bf16[1024,128]{1,0:T(8,128)(2,1)}, u32[]{:S(2)}) copy-start(bf16[1024,128]{1,0:T(8,128)(2,1)} %param.9) | copy-start | bytes 786436
  0.6 1.5 %copy-start.2 = (s32[1024,1]{0,1:T(1,128)S(1)}, s32[1024,1]{0,1:T(1,128)}, u32[]{:S(2)}) copy-start(s32[1024,1]{0,1:T(1,128)} %param.7) | copy-start | bytes 12292
  0.7 1.5 %copy-start.4 = (s32[1024]{0:T(1024)S(1)}, s32[1024]{0:T(1024)}, u32[]{:S(2)}) copy-start(s32[1024]{0:T(1024)} %param.8) | copy-start | bytes 12292
  1.5 1.7 %copy-start.5 = (s32[1024]{0:T(1024)S(1)}, s32[1024]{0:T(1024)}, u32[]{:S(2)}) copy-start(s32[1024]{0:T(1024)} %param.13) | copy-start | bytes 12292
  2.1 1.8 %copy-start.3 = (s32[1024,1]{0,1:T(1,128)S(1)}, s32[1024,1]{0,1:T(1,128)}, u32[]{:S(2)}) copy-start(s32[1024,1]{0,1:T(1,128)} %param.12) | copy-start | bytes 12292
  7.1 36.7 %copy-start.1 = (f32[8192]{0:T(1024)S(1)}, f32[8192]{0:T(1024)}, u32[]{:S(2)}) copy-start(f32[8192]{0:T(1024)} %param.11) | copy-start | bytes 98308
  64.5 28.9 %all-to-all-start.1 = ((bf16[32,128,128]{2,1,0:T(8,128)(2,1)}), bf16[32,128,128]{2,1,0:T(8,128)(2,1)S(1)}, u32[]{:S(2)}, u32[]{:S(2)}) async-start(bf16[32,128,128]{2,1,0:T(8,128)(2,1)} %bitcast.9), calls=%async_computation.1 | async-start | bytes 2097152 | tf_op jit(solution)/shard_map/all_to_all | solution.py:196

commit v3 on v2

--- a/solution.py
+++ b/solution.py
@@ -70,7 +70,7 @@
                 (zero_rows, LANES), jnp.float32
             )
 
-    group = 32 if capacity % 32 == 0 else 8
+    group = next(size for size in (64, 32, 8) if capacity % size == 0)
     per_block = capacity // group
     rows_load.wait()
 
@@ -91,7 +91,7 @@
     load.wait()
     for piece in range(chunks):
 
-        @pl.loop(0, chunk // LANES, unroll=2)
+        @pl.loop(0, chunk // LANES, unroll=4)
         def _(step):
             tile = piece * (chunk // LANES) + step
             span = pl.ds(pl.multiple_of(tile * LANES, LANES), LANES)

time: 97.2 us -> 94.7 us (0.974)
  Pallas kernels: 20.7 us -> 18.4 us
    pallas_call x1, Pallas kernels: 20.7 us -> 18.4 us  [update(): pl.pallas_call(update_kernel, name='update', out_shape=(jax.ShapeDtypeStr...]
where the time goes in v3:
time: 94.7 us; the launch traced here: 94.6 us
  blocking collectives  36.5 us (39%)
  waiting for transfers between devices  26.2 us (28%)
  Pallas kernels  18.4 us (19%)
  matrix products  7.5 us (8%)
  starting transfers between devices  2.66 us (3%)
  other arithmetic  2.37 us (3%)
    all_to_all x1, blocking collectives, on_device(): lax.all_to_all(outgoing, axes, split_axis=0, concat_axis=0, tiled=True)  36.5 us
    all_to_all x1, waiting for transfers between devices, on_device(): lax.all_to_all(fetched.reshape(devices, capacity, columns), axes, split_a...  26.2 us
    pallas_call x1, Pallas kernels, update(): pl.pallas_call(update_kernel, name='update', out_shape=(jax.ShapeDtypeStr...  18.4 us
    dot_general x1, matrix products, on_device(): jnp.dot((next_places[:, None] == slot_index[None, :]).astype(jnp.bfloat16...  3.51 us
    dot_general x1, matrix products, on_device(): jnp.dot((slot_index[:, None] == places[None, :]).astype(jnp.bfloat16), gr...  2.95 us
    all_to_all x1, starting transfers between devices, on_device(): lax.all_to_all(fetched.reshape(devices, capacity, columns), axes, split_a...  2.66 us
  transfers between devices with their start and end apart: 1, of which 1 were waited for; matrix products, arithmetic and copies ran while one was open for 0% of the time, Pallas kernels for 0%

profile of v3, /device:TPU:0, one launch (start us, length us, event | category | flops | bytes accessed | tf_op | source)
XLA Modules:
  0.0 94.6 jit_solution(10140560453087424178)
XLA Ops:
  0.6 0.0 copy-start
  0.6 0.0 copy-start.2
  0.7 0.0 copy-start.4
  0.7 0.8 iota_compare_fusion.15
  1.5 0.0 copy-start.5
  1.5 0.6 fusion.7
  2.1 0.0 copy-start.3
  2.1 0.0 copy-done.2
  2.1 0.0 copy-done.4
  2.2 0.2 select_convert_fusion.3
  2.4 0.5 select_convert_fusion.5
  2.9 0.2 fusion.8
  3.1 0.0 copy-done.5
  3.2 0.2 select_convert_fusion
  3.4 0.5 select_convert_fusion.2
  3.8 0.0 copy-done.3
  3.8 0.2 fusion.14
  4.1 0.0 copy-done
  4.1 2.9 %fusion.4 = bf16[4096,128]{1,0:T(8,128)(2,1)S(1)} fusion(bf16[1024,128]{1,0:T(8,128)(2,1)S(1)} %copy-done, s32[1024]{0:T(1024)S(1)} %multiply_add_fusion.1), kind=kOutput, calls=%fused_computation.6 | convolution fusion | flops 1078460416 | bytes 1314816 | tf_op jit(solution)/shard_map/dot_general | solution.py:182
  7.1 0.0 copy-start.1
  7.1 0.1 pad_maximum_fusion
  7.2 36.5 %all_to_all.10.incoming_ref = bf16[32,136,128]{2,1,0:T(8,128)(2,1)S(1)} all-to-all(bf16[32,136,128]{2,1,0:T(8,128)(2,1)S(1)} %pad_maximum_fusion), channel_id=1, replica_groups=mesh['dp'=4,'rows'=8] {'dp','rows'}, dimensions={0} | all-to-all | bytes 2228224 | tf_op jit(solution)/shard_map/all_to_all | solution.py:190
  43.8 0.0 copy-done.1
  43.8 18.4 %update.1 = (f32[8192,128]{1,0:T(8,128)}, f32[64,128]{1,0:T(8,128)}, bf16[4096,128]{1,0:T(8,128)(2,1)}) custom-call(s32[4096]{0:T(1024)S(1)} %bitcast.21, s32[4096]{0:T(1024)S(1)} %bitcast.20, bf16[32,136,128]{2,1,0:T(8,128)(2,1)S(1)} %all_to_all.10.incoming_ref, f32[8192,128]{1,0:T(8,128)} %embedding_ref.1, f32[64,128]{1,0:T(8,128)S(1)} %bitcast.22), custom_call_target="tpu_custom_call" | custom-call | tf_op jit(solution)/shard_map/update/pallas_call | solution.py:138
  62.2 2.7 %all-to-all-start.1 = ((bf16[32,128,128]{2,1,0:T(8,128)(2,1)}), bf16[32,128,128]{2,1,0:T(8,128)(2,1)S(1)}, u32[]{:S(2)}, u32[]{:S(2)}) async-start(bf16[32,128,128]{2,1,0:T(8,128)(2,1)} %bitcast.9), calls=%async_computation.1 | async-start | bytes 2097152 | tf_op jit(solution)/shard_map/all_to_all | solution.py:196
  64.9 26.2 %all-to-all-done.1 = bf16[32,128,128]{2,1,0:T(8,128)(2,1)S(1)} async-done(((bf16[32,128,128]{2,1,0:T(8,128)(2,1)}), bf16[32,128,128]{2,1,0:T(8,128)(2,1)S(1)}, u32[]{:S(2)}, u32[]{:S(2)}) %all-to-all-start.1) | async-done | bytes 1048608 | tf_op jit(solution)/shard_map/all_to_all | solution.py:196
  91.1 3.5 %fusion.6 = bf16[1024,128]{1,0:T(8,128)(2,1)} fusion(bf16[4096,128]{1,0:T(8,128)(2,1)S(1)} %bitcast.23, s32[1024]{0:T(1024)S(1)} %bitcast.34), kind=kOutput, calls=%fused_computation.9 | convolution fusion | flops 1078067200 | bytes 1314816 | tf_op jit(solution)/shard_map/dot_general | solution.py:199
  (17 shorter events, 0.2 us)
Async XLA Ops:
  0.6 3.5 %copy-start = (bf16[1024,128]{1,0:T(8,128)(2,1)S(1)}, bf16[1024,128]{1,0:T(8,128)(2,1)}, u32[]{:S(2)}) copy-start(bf16[1024,128]{1,0:T(8,128)(2,1)} %param.9) | copy-start | bytes 786436
  0.6 1.5 %copy-start.2 = (s32[1024,1]{0,1:T(1,128)S(1)}, s32[1024,1]{0,1:T(1,128)}, u32[]{:S(2)}) copy-start(s32[1024,1]{0,1:T(1,128)} %param.7) | copy-start | bytes 12292
  0.7 1.5 %copy-start.4 = (s32[1024]{0:T(1024)S(1)}, s32[1024]{0:T(1024)}, u32[]{:S(2)}) copy-start(s32[1024]{0:T(1024)} %param.8) | copy-start | bytes 12292
  1.5 1.7 %copy-start.5 = (s32[1024]{0:T(1024)S(1)}, s32[1024]{0:T(1024)}, u32[]{:S(2)}) copy-start(s32[1024]{0:T(1024)} %param.13) | copy-start | bytes 12292
  2.1 1.8 %copy-start.3 = (s32[1024,1]{0,1:T(1,128)S(1)}, s32[1024,1]{0,1:T(1,128)}, u32[]{:S(2)}) copy-start(s32[1024,1]{0,1:T(1,128)} %param.12) | copy-start | bytes 12292
  7.1 36.7 %copy-start.1 = (f32[8192]{0:T(1024)S(1)}, f32[8192]{0:T(1024)}, u32[]{:S(2)}) copy-start(f32[8192]{0:T(1024)} %param.11) | copy-start | bytes 98308
  62.2 28.9 %all-to-all-start.1 = ((bf16[32,128,128]{2,1,0:T(8,128)(2,1)}), bf16[32,128,128]{2,1,0:T(8,128)(2,1)S(1)}, u32[]{:S(2)}, u32[]{:S(2)}) async-start(bf16[32,128,128]{2,1,0:T(8,128)(2,1)} %bitcast.9), calls=%async_computation.1 | async-start | bytes 2097152 | tf_op jit(solution)/shard_map/all_to_all | solution.py:196
